TPU v7x, 32 devices: a whole 2x2x4 slice. The times are simulated.
32 devices in a mesh: expert: 8 (over z, y), gate: 4 (over x, core).
Axes of the slice: x: 2, y: 2, z: 4, core: 2. Of those that a mesh axis runs over, the one named last changes fastest.
Arguments:
- samples: bfloat16 [6144, 4096], P('expert', 'gate'), may hold values from -4 to 4
- gate_weight: bfloat16 [4096, 32], P('gate'), may hold values from -1 to 1
- expert_ids: int32 [6144, 2], P('expert'), may hold values from 0 to 31, all different within a row; in each aligned block of 768 rows (0 to 767, 768 to 1535, ...) at most 96 rows name the same one
- pad_mask: int32 [6144], P('expert'), may hold values 0 or 1
- up_weight: bfloat16 [32, 4096, 1024], P(('expert', 'gate')), may hold values from -0.09375 to 0.09375
- down_weight: bfloat16 [32, 1024, 1024], P(('expert', 'gate')), may hold values from -0.1875 to 0.1875
Outputs:
- combined: bfloat16 [6144, 1024], P('expert', 'gate')
Inputs may be any that keep to these rules, and one draw needn't show every extreme that they name: `expert_ids`: each sample names two different experts; among the 768 samples of one index of expert no expert is named more than 96 times, a bound that some block reaches.
All inputs are finite; a program needn't handle non-finite values. No bound on the sum of `pad_mask` on one device may be relied on, other than what follows from the above.
Results may differ from a plain program's by a relative error of at most 0.0057.
Values may be sent and summed in bfloat16 or wider, within the bound.
A program may use at most 128 MiB of HBM per device.

v0:
```python
import jax
import jax.numpy as jnp
from jax import lax
from jax.sharding import PartitionSpec as P


def joined(shard, axis, combine):
    everything = jax.tree.map(lambda part: lax.all_gather(part, axis), shard)
    leading = jax.tree.map(lambda part: part[0], everything)

    def step(k, so_far):
        return combine(so_far, jax.tree.map(lambda part: part[k], everything))

    return lax.fori_loop(1, lax.axis_size(axis), step, leading)


def combine_parts(first, second):
    row_top = jnp.maximum(first[0], second[0])
    left_scale = jnp.exp(first[0] - row_top)
    right_scale = jnp.exp(second[0] - row_top)
    row_total = first[1] * left_scale + second[1] * right_scale
    chosen = first[2] * left_scale[None, :] + second[2] * right_scale[None, :]
    return (row_top, row_total, chosen)


def per_device(samples, gate_weight, expert_ids, pad_mask, up_weight, down_weight):
    row_count = samples.shape[0]
    group_count = lax.axis_size("expert")
    gate_count = lax.axis_size("gate")
    expert_count = group_count * gate_count
    capacity = 4 * row_count // expert_count
    col_count = expert_count // gate_count
    gate_index = lax.axis_index("gate")
    logits_t = lax.psum_scatter(
        lax.dot_general(
            gate_weight, samples, (((0,), (1,)), ((), ())), preferred_element_type=jnp.float32
        ),
        "gate",
        scatter_dimension=0,
        tiled=True,
    )
    flat_ids = expert_ids.reshape(-1)
    onehot = (flat_ids[:, None] == jnp.arange(expert_count, dtype=jnp.int32)[None, :]).astype(
        jnp.int32
    )
    slot_rank = jnp.sum(onehot * (jnp.cumsum(onehot, axis=0) - 1), axis=1)
    position = flat_ids * capacity + slot_rank
    row_index = jnp.repeat(jnp.arange(row_count, dtype=jnp.int32), 2)
    owners = jnp.full((expert_count * capacity,), row_count, jnp.int32).at[position].set(row_index)
    whole_rows = lax.all_gather(samples, "gate", axis=1, tiled=True)
    padded = jnp.concatenate(
        [whole_rows, jnp.zeros((1, whole_rows.shape[1]), whole_rows.dtype)], axis=0
    )
    column_owners = lax.dynamic_index_in_dim(
        owners.reshape(group_count, gate_count, capacity), gate_index, 1, keepdims=False
    )
    outgoing = padded[column_owners]
    incoming = lax.all_to_all(outgoing, "expert", split_axis=0, concat_axis=0, tiled=True)
    slot_rows = incoming.reshape(group_count * capacity, whole_rows.shape[1])
    hidden = jnp.dot(slot_rows, up_weight[0], preferred_element_type=jnp.float32)
    active = jnp.maximum(hidden, 0.0).astype(jnp.bfloat16)
    expert_out = jnp.dot(active, down_weight[0], preferred_element_type=jnp.float32).astype(
        jnp.bfloat16
    )
    out_share = expert_out.shape[1] // gate_count
    outbound = expert_out.reshape(group_count, 1, 1, capacity, gate_count, out_share)
    returned = lax.all_to_all(
        lax.all_to_all(outbound, "expert", split_axis=0, concat_axis=1, tiled=True),
        "gate",
        split_axis=4,
        concat_axis=2,
        tiled=True,
    )
    returned = returned.reshape(expert_count * capacity, out_share)
    offset = expert_ids - gate_index * col_count
    inside = ((offset >= 0) & (offset < col_count)).T
    chosen = jnp.take_along_axis(logits_t, jnp.clip(offset, 0, col_count - 1).T, axis=0)
    local_top = jnp.max(logits_t, axis=0)
    local_total = jnp.sum(jnp.exp(logits_t - local_top[None, :]), axis=0)
    local_chosen = jnp.where(inside, jnp.exp(chosen - local_top[None, :]), 0.0)
    row_top, row_total, numerator = joined(
        (local_top, local_total, local_chosen), "gate", combine_parts
    )
    factor = expert_count * numerator / row_total[None, :] * pad_mask.astype(jnp.float32)[None, :]
    picked = returned[position].astype(jnp.float32).reshape(row_count, 2, out_share)
    mixed = factor[0][:, None] * picked[:, 0, :] + factor[1][:, None] * picked[:, 1, :]
    return mixed.astype(jnp.bfloat16)


def solution(mesh):
    placed = (
        P("expert", "gate"),
        P("gate", None),
        P("expert", None),
        P("expert"),
        P(("expert", "gate"), None, None),
        P(("expert", "gate"), None, None),
    )
    return jax.shard_map(
        per_device, mesh=mesh, in_specs=placed, out_specs=P("expert", "gate"), check_vma=False
    )
```

profile of v0, /device:TPU:31, one launch (start us, length us, event | category | flops | bytes accessed | tf_op | source)
XLA Modules:
  0.0 342.3 jit_solution(15891063067835120710)
XLA Ops:
  7.3 0.9 copy.19
  9.8 9.1 %reduce-window.6 = s32[32,12,128]{2,1,0:T(8,128)S(1)} reduce-window(s32[32,12,128]{2,1,0:T(8,128)S(1)} %fusion.14, s32[]{:T(128)} %constant.77.clone.1), window={size=1x1x128 pad=0_0x0_0x127_0}, to_apply=%region_5.6 | reduce-window | flops 6242304 | bytes 393220 | tf_op jit(solution)/shard_map/reduce-window
  19.8 6.2 %scatter_custom_fusion = s32[3072]{0:T(1024)S(1)} fusion(s32[1536]{0:T(1024)S(1)} %fusion.17, s32[1536]{0:T(1024)S(1)} %reshape.149, s32[]{:T(128)} %constant.86.clone.1), kind=kCustom, calls=%fused_computation.44 | custom fusion | bytes 12292 | tf_op jit(solution)/shard_map/scatter | solution.py:49
  26.2 29.5 %all-gather.8.cloned.1.call-done = bf16[768,4096]{1,0:T(8,128)(2,1)} async-done(((bf16[768,1024]{1,0:T(8,128)(2,1)}), bf16[768,4096]{1,0:T(8,128)(2,1)}) %all-gather.8.cloned.1.call-update) | async-done | bytes 6291472 | tf_op jit(solution)/shard_map/all_gather | solution.py:50
  55.7 6.2 %concatenate.3 = bf16[769,4096]{1,0:T(8,128)(2,1)} pad(bf16[768,4096]{1,0:T(8,128)(2,1)} %all-gather.8.cloned.1.call-done, bf16[]{:T(256)} %constant.85.clone.1), padding=0_1x0_0 | pad | bytes 12591106 | tf_op jit(solution)/shard_map/concatenate | solution.py:51
  62.0 15.6 %gather_fusion = bf16[768,4096]{1,0:T(8,128)(2,1)} fusion(bf16[769,4096]{1,0:T(8,128)(2,1)} %concatenate.3, s32[1024]{0:T(1024)S(1)} %pad_clamp_fusion.1), kind=kCustom, calls=%fused_computation | custom fusion | bytes 12585984 | tf_op jit(solution)/shard_map/gather | solution.py:57
  77.5 141.8 %all_to_all.32 = bf16[8,96,4096]{2,1,0:T(8,128)(2,1)} all-to-all(bf16[8,96,4096]{2,1,0:T(8,128)(2,1)} %bitcast.93), channel_id=1, replica_groups=mesh['expert'=8,'gate'=4] {'expert'}, dimensions={0} | all-to-all | bytes 12582912 | tf_op jit(solution)/shard_map/all_to_all | solution.py:58
  219.3 14.6 %fusion.7 = bf16[768,1024]{1,0:T(8,128)(2,1)} fusion(bf16[1,1024,1024]{2,1,0:T(8,128)(2,1)S(1)} %copy-done, bf16[768,4096]{1,0:T(8,128)(2,1)} %bitcast.94, bf16[1,4096,1024]{2,1,0:T(8,128)(2,1)} %param.12), kind=kOutput, calls=%fused_computation.16 | convolution fusion | flops 8055422976 | bytes 18350080 | tf_op jit(solution)/shard_map/dot_general | solution.py:62
  233.9 3.9 %reshape.120 = bf16[8,1,1,96,4,256]{5,4,3,0,2,1:T(4,128)(2,1)} reshape(bf16[768,1024]{1,0:T(8,128)(2,1)} %fusion.7) | data formatting | bytes 3145728 | tf_op jit(solution)/shard_map/reshape | solution.py:66
  237.9 5.6 %all-to-all-start.1 = ((bf16[8,1,1,96,4,256]{5,4,3,2,1,0:T(4,128)(2,1)}), bf16[8,1,1,96,4,256]{5,4,3,2,1,0:T(4,128)(2,1)}, u32[]{:S(2)}, u32[]{:S(2)}) async-start(bf16[8,1,1,96,4,256]{5,4,3,2,1,0:T(4,128)(2,1)} %bitcast.95), calls=%async_computation.2 | async-start | bytes 3145728 | tf_op jit(solution)/shard_map/all_to_all | solution.py:68
  243.4 2.6 fusion.23
  246.2 20.7 %reduce-scatter.2.cloned.1.call-done = f32[8,768]{1,0:T(8,128)} async-done(((f32[32,768]{1,0:T(8,128)}), f32[8,768]{1,0:T(8,128)}) %reduce-scatter.2.cloned.1.call-update) | async-done | bytes 24592 | tf_op jit(solution)/shard_map/reduce_scatter | solution.py:34
  268.5 9.4 %gather_fusion.2 = f32[1536]{0:T(1024)S(1)} fusion(f32[8,768]{1,0:T(8,128)S(1)} %copy-done.1, s32[1536]{0:T(1024)S(1)} %reshape.139), kind=kCustom, calls=%fused_computation.2 | custom fusion | bytes 24576 | tf_op jit(solution)/shard_map/jit(take_along_axis)/gather | solution.py:77
  277.9 6.3 %all-gather.3 = f32[4,1,768]{2,1,0:T(1,128)S(1)} all-gather(f32[1,1,768]{2,1,0:T(1,128)S(1)} %reshape.168), channel_id=2, replica_groups=mesh['expert'=8,'gate'=4] {'gate'}, dimensions={0}, use_global_device_ids=true | all-gather | bytes 15360 | tf_op jit(solution)/shard_map/all_gather | solution.py:8
  284.2 5.2 %all-gather.4 = f32[4,1,768]{2,1,0:T(1,128)S(1)} all-gather(f32[1,1,768]{2,1,0:T(1,128)S(1)} %reshape.170), channel_id=3, replica_groups=mesh['expert'=8,'gate'=4] {'gate'}, dimensions={0}, use_global_device_ids=true | all-gather | bytes 15360 | tf_op jit(solution)/shard_map/all_gather | solution.py:8
  289.4 5.2 %all-gather.5 = f32[4,2,768]{2,1,0:T(2,128)S(1)} all-gather(f32[1,2,768]{2,1,0:T(2,128)S(1)} %fusion.19), channel_id=4, replica_groups=mesh['expert'=8,'gate'=4] {'gate'}, dimensions={0}, use_global_device_ids=true | all-gather | bytes 30720 | tf_op jit(solution)/shard_map/all_gather | solution.py:8
  294.6 2.8 copy.24
  297.5 5.5 %all-to-all-start.2 = ((bf16[1,8,1,96,4,256]{5,3,1,2,0,4:T(8,128)(2,1)}), bf16[1,8,1,96,4,256]{5,3,1,2,0,4:T(8,128)(2,1)}, u32[]{:S(2)}, u32[]{:S(2)}) async-start(bf16[1,8,1,96,4,256]{5,3,1,2,0,4:T(8,128)(2,1)} %copy.24), calls=%async_computation.3 | async-start | bytes 3145728 | tf_op jit(solution)/shard_map/all_to_all | solution.py:67
  303.3 18.0 %all-to-all-done.2 = bf16[1,8,1,96,4,256]{5,3,1,2,0,4:T(8,128)(2,1)} async-done(((bf16[1,8,1,96,4,256]{5,3,1,2,0,4:T(8,128)(2,1)}), bf16[1,8,1,96,4,256]{5,3,1,2,0,4:T(8,128)(2,1)}, u32[]{:S(2)}, u32[]{:S(2)}) %all-to-all-start.2) | async-done | bytes 1572896 | tf_op jit(solution)/shard_map/all_to_all | solution.py:67
  321.3 2.7 copy.25
  324.0 5.3 %gather_fusion.1 = bf16[1536,256]{1,0:T(8,128)(2,1)S(1)} fusion(bf16[3072,256]{1,0:T(8,128)(2,1)} %bitcast.92, s32[2048]{0:T(1024)S(1)} %pad_clamp_fusion), kind=kCustom, calls=%fused_computation.1 | custom fusion | bytes 1579008 | tf_op jit(solution)/shard_map/gather | solution.py:85
  329.2 1.9 reshape.122
  331.2 3.3 fusion.22
  334.4 1.0 fusion.12
  (62 shorter events, 5.6 us)
Async XLA Ops:
  6.5 212.8 %copy-start = (bf16[1,1024,1024]{2,1,0:T(8,128)(2,1)S(1)}, bf16[1,1024,1024]{2,1,0:T(8,128)(2,1)}, u32[]{:S(2)}) copy-start(bf16[1,1024,1024]{2,1,0:T(8,128)(2,1)} %param.13) | copy-start | bytes 6291460
  6.5 49.2 %all-gather.8.cloned.1.call-start = ((), (), s32[]{:S(2)}) async-start(), calls=%async_computation.5 | async-start | bytes 7864320 | tf_op jit(solution)/shard_map/all_gather | solution.py:50
  233.9 9.5 %copy-start.3 = (bf16[1024,32]{0,1:T(8,128)(2,1)S(1)}, bf16[1024,32]{0,1:T(8,128)(2,1)}, u32[]{:S(2)}) copy-start(bf16[1024,32]{0,1:T(8,128)(2,1)} %param.9) | copy-start | bytes 196612
  237.9 8.2 %copy-start.2 = (s32[768,2]{0,1:T(2,128)S(1)}, s32[768,2]{0,1:T(2,128)}, u32[]{:S(2)}) copy-start(s32[768,2]{0,1:T(2,128)} %param.10) | copy-start | bytes 18436
  237.9 8.3 %copy-start.4 = (s32[768]{0:T(1024)S(1)}, s32[768]{0:T(1024)}, u32[]{:S(2)}) copy-start(s32[768]{0:T(1024)} %param.11) | copy-start | bytes 9220
  237.9 56.8 %all-to-all-start.1 = ((bf16[8,1,1,96,4,256]{5,4,3,2,1,0:T(4,128)(2,1)}), bf16[8,1,1,96,4,256]{5,4,3,2,1,0:T(4,128)(2,1)}, u32[]{:S(2)}, u32[]{:S(2)}) async-start(bf16[8,1,1,96,4,256]{5,4,3,2,1,0:T(4,128)(2,1)} %bitcast.95), calls=%async_computation.2 | async-start | bytes 3145728 | tf_op jit(solution)/shard_map/all_to_all | solution.py:68
  243.4 23.5 %reduce-scatter.2.cloned.1.call-start = ((), (), s32[]{:S(2)}) async-start(), calls=%async_computation.4 | async-start | bytes 122880 | tf_op jit(solution)/shard_map/reduce_scatter | solution.py:34
  266.9 1.6 copy-start.1
  297.5 23.8 %all-to-all-start.2 = ((bf16[1,8,1,96,4,256]{5,3,1,2,0,4:T(8,128)(2,1)}), bf16[1,8,1,96,4,256]{5,3,1,2,0,4:T(8,128)(2,1)}, u32[]{:S(2)}, u32[]{:S(2)}) async-start(bf16[1,8,1,96,4,256]{5,3,1,2,0,4:T(8,128)(2,1)} %copy.24), calls=%async_computation.3 | async-start | bytes 3145728 | tf_op jit(solution)/shard_map/all_to_all | solution.py:67
Sparse Core Ops, SparseCore 0:
  8.9 46.7 all-gather.7
  246.7 20.1 reduce-scatter.1
where the time goes:
time: 346 us; the launch traced here: 342 us
  blocking collectives  158 us (46%)
  waiting for transfers between devices  68.9 us (20%)
  local copies, waits for them, and re-layouts  60 us (17%)
  matrix products  17.2 us (5%)
  between operations  13.7 us (4%)
  other arithmetic  12.8 us (4%)
  starting transfers between devices  11.1 us (3%)
    all_to_all x1, blocking collectives, per_device(): lax.all_to_all(outgoing, 'expert', split_axis=0, concat_axis=0, tiled=True)  142 us
    all_gather x1, waiting for transfers between devices, per_device(): whole_rows = lax.all_gather(samples, 'gate', axis=1, tiled=True)  29.5 us
    reduce_scatter x1, waiting for transfers between devices, per_device(): lax.psum_scatter(lax.dot_general(gate_weight, samples, (((0,), (1,)), (()...  20.7 us
    all_to_all x1, waiting for transfers between devices, per_device(): lax.all_to_all(lax.all_to_all(outbound, 'expert', split_axis=0, concat_ax...  18 us
    all_gather x3, blocking collectives, joined(): everything = jax.tree.map(lambda part: lax.all_gather(part, axis), shard)  16.6 us
    gather x1, local copies, waits for them, and re-layouts, per_device(): outgoing = padded[column_owners]  15.6 us
    dot_general x1, matrix products, per_device(): jnp.dot(active, down_weight[0], preferred_element_type=jnp.float32)  14.6 us
    gather x3, local copies, waits for them, and re-layouts, per_device(): jnp.take_along_axis(logits_t, jnp.clip(offset, 0, col_count - 1).T, axis=0)  9.39 us
  transfers between devices with their start and end apart: 4, of which 3 were waited for; matrix products, arithmetic and copies ran while one was open for 10% of the time, Pallas kernels for 0%

commit v1 on v0

v1 whole, which is shorter than its diff:
```python
import jax
import jax.numpy as jnp
from jax import lax
from jax.sharding import PartitionSpec as P


def routing(expert_ids, expert_count):
    row_count = expert_ids.shape[0]
    lanes = jnp.arange(expert_count, dtype=jnp.int32)[None, :]
    first = expert_ids[:, 0:1] == lanes
    second = expert_ids[:, 1:2] == lanes
    member = first | second
    rows = jnp.arange(row_count, dtype=jnp.int32)
    lower = (rows[:, None] > rows[None, :]).astype(jnp.bfloat16)
    before = jnp.dot(lower, member.astype(jnp.bfloat16), preferred_element_type=jnp.float32)
    before = before.astype(jnp.int32)
    return first, second, member, before


def factors(logits, first, second, pad_mask, expert_count):
    top = jnp.max(logits, axis=1, keepdims=True)
    terms = jnp.exp(logits - top)
    scale = pad_mask.astype(jnp.float32)[:, None] / jnp.sum(terms, axis=1, keepdims=True)
    factor0 = expert_count * jnp.sum(jnp.where(first, terms, 0.0), axis=1, keepdims=True) * scale
    factor1 = expert_count * jnp.sum(jnp.where(second, terms, 0.0), axis=1, keepdims=True) * scale
    return factor0, factor1


def per_device(samples, gate_weight, expert_ids, pad_mask, up_weight, down_weight):
    row_count, share = samples.shape
    group_count = lax.axis_size("expert")
    gate_count = lax.axis_size("gate")
    expert_count = group_count * gate_count
    capacity = 4 * row_count // expert_count
    partial = jnp.dot(samples, gate_weight, preferred_element_type=jnp.float32)
    logits = jnp.sum(lax.all_gather(partial, "gate"), axis=0)
    first, second, member, before = routing(expert_ids, expert_count)
    place = jnp.where(member, before, -1).T
    ranks = jnp.arange(capacity, dtype=jnp.int32)
    send = (place[:, None, :] == ranks[None, :, None]).astype(jnp.bfloat16)
    outgoing = jnp.dot(
        send.reshape(expert_count * capacity, row_count), samples, preferred_element_type=jnp.float32
    ).astype(jnp.bfloat16)
    incoming = lax.all_to_all(
        outgoing.reshape(expert_count, capacity, share),
        ("expert", "gate"),
        split_axis=0,
        concat_axis=0,
        tiled=True,
    ).reshape(group_count, gate_count, capacity, share)
    hidden = 0.0
    for g in range(gate_count):
        hidden += jnp.dot(
            incoming[:, g].reshape(group_count * capacity, share),
            up_weight[0, g * share : (g + 1) * share],
            preferred_element_type=jnp.float32,
        )
    active = jnp.maximum(hidden, 0.0).astype(jnp.bfloat16)
    expert_out = jnp.dot(active, down_weight[0], preferred_element_type=jnp.float32).astype(
        jnp.bfloat16
    )
    out_share = expert_out.shape[1] // gate_count
    outbound = expert_out.reshape(group_count, capacity, gate_count, out_share)
    outbound = outbound.transpose(0, 2, 1, 3).reshape(expert_count, capacity, out_share)
    returned = lax.all_to_all(
        outbound, ("expert", "gate"), split_axis=0, concat_axis=0, tiled=True
    ).reshape(expert_count * capacity, out_share)
    factor0, factor1 = factors(logits, first, second, pad_mask, expert_count)
    slots = jnp.arange(expert_count * capacity, dtype=jnp.int32)[None, :]
    mixed = 0.0
    for k, (chosen, factor) in enumerate(((first, factor0), (second, factor1))):
        rank = jnp.sum(jnp.where(chosen, before, 0), axis=1, keepdims=True)
        position = expert_ids[:, k : k + 1] * capacity + rank
        pick = (position == slots).astype(jnp.bfloat16)
        mixed += factor * jnp.dot(pick, returned, preferred_element_type=jnp.float32)
    return mixed.astype(jnp.bfloat16)


def solution(mesh):
    placed = (
        P("expert", "gate"),
        P("gate", None),
        P("expert", None),
        P("expert"),
        P(("expert", "gate"), None, None),
        P(("expert", "gate"), None, None),
    )
    return jax.shard_map(
        per_device, mesh=mesh, in_specs=placed, out_specs=P("expert", "gate"), check_vma=False
    )
```

time: 346 us -> 232 us (0.67)
  waiting for transfers between devices: 68.9 us -> 18.2 us
  local copies, waits for them, and re-layouts: 60 us -> 10.7 us
  matrix products: 17.2 us -> 34.6 us
  between operations: 13.7 us -> 0.17 us
  other arithmetic: 12.8 us -> 1.76 us
  starting transfers between devices: 11.1 us -> 5.94 us
    gather x5 -> x0, local copies, waits for them, and re-layouts: 30.2 us -> none  [the longest x1 15.6 us: per_device(): outgoing = padded[column_owners]]
    all_gather x1 -> x0, waiting for transfers between devices: 29.5 us -> none  [per_device(): whole_rows = lax.all_gather(samples, 'gate', axis=1, tiled=True)]
    dot_general x1 -> x8, matrix products: 2.62 us -> 25.1 us  [the longest x3 10.5 us: per_device(): jnp.dot(incoming[:, g].reshape(group_count * capacity, share), up_weight[...]
    reduce_scatter x1 -> x0, waiting for transfers between devices: 20.7 us -> none  [per_device(): lax.psum_scatter(lax.dot_general(gate_weight, samples, (((0,), (1,)), (()...]
    another operation x2 -> x0, other arithmetic: 9.11 us -> none
    concatenate x1 -> x0, local copies, waits for them, and re-layouts: 6.24 us -> none  [per_device(): jnp.concatenate([whole_rows, jnp.zeros((1, whole_rows.shape[1]), whole_ro...]
    scatter x1 -> x0, local copies, waits for them, and re-layouts: 6.19 us -> none  [per_device(): jnp.full((expert_count * capacity,), row_count, jnp.int32).at[position]]
    all_to_all x2 -> x0, local copies, waits for them, and re-layouts: 5.51 us -> none  [the longest x1 2.83 us: per_device(): lax.all_to_all(outbound, 'expert', split_axis=0, concat_axis=1, tiled=True)]
  transfers between devices with their start and end apart: 4 -> 1, of which waited for: 3 -> 1; matrix products, arithmetic and copies ran while one was open for 10% -> 1% of each run, Pallas kernels for 0% -> 0%
where the time goes in v1:
time: 232 us; the launch traced here: 228 us
  blocking collectives  157 us (68%)
  matrix products  34.6 us (15%)
  waiting for transfers between devices  18.2 us (8%)
  local copies, waits for them, and re-layouts  10.7 us (5%)
  starting transfers between devices  5.94 us (3%)
    all_to_all x1, blocking collectives, per_device(): lax.all_to_all(outgoing.reshape(expert_count, capacity, share), ('expert'...  142 us
    all_to_all x1, waiting for transfers between devices, per_device(): lax.all_to_all(outbound, ('expert', 'gate'), split_axis=0, concat_axis=0,...  18.2 us
    all_gather x1, blocking collectives, per_device(): logits = jnp.sum(lax.all_gather(partial, 'gate'), axis=0)  14.8 us
    dot_general x3, matrix products, per_device(): jnp.dot(incoming[:, g].reshape(group_count * capacity, share), up_weight[...  10.5 us
    dot_general x1, matrix products, per_device(): jnp.dot(active, down_weight[0], preferred_element_type=jnp.float32)  9.54 us
    dot_general x2, matrix products, per_device(): jnp.dot(pick, returned, preferred_element_type=jnp.float32)  7.01 us
    reshape x2, local copies, waits for them, and re-layouts, per_device(): outbound = expert_out.reshape(group_count, capacity, gate_count, out_share)  6.73 us
    all_to_all x1, starting transfers between devices, per_device(): lax.all_to_all(outbound, ('expert', 'gate'), split_axis=0, concat_axis=0,...  5.94 us
  transfers between devices with their start and end apart: 1, of which 1 were waited for; matrix products, arithmetic and copies ran while one was open for 1% of the time, Pallas kernels for 0%

profile of v1, /device:TPU:31, one launch (start us, length us, event | category | flops | bytes accessed | tf_op | source)
XLA Modules:
  0.0 228.4 jit_solution(5764455096693125479)
XLA Ops:
  0.0 0.9 slice_reduce_fusion.1
  0.9 0.1 eq.115
  1.0 0.4 bitcast_select_fusion
  1.3 1.4 bitcast_compare_fusion
  2.7 5.3 %convolution_convert_fusion = bf16[3072,1024]{1,0:T(8,128)(2,1)S(1)} fusion(pred[3072,768]{1,0:T(32,128)(4,1)S(1)} %bitcast_compare_fusion, bf16[768,1024]{1,0:T(8,128)(2,1)S(1)} %copy-done.1), kind=kOutput, calls=%fused_computation.5 | convolution fusion | flops 4834983936 | bytes 10223616 | tf_op jit(solution)/shard_map/dot_general | solution.py:41
  8.0 0.0 slice-start
  8.0 142.3 %all_to_all.10 = bf16[32,96,1024]{2,1,0:T(8,128)(2,1)S(1)} all-to-all(bf16[32,96,1024]{2,1,0:T(8,128)(2,1)S(1)} %bitcast.48), channel_id=1, replica_groups=mesh['expert'=8,'gate'=4] {'expert','gate'}, dimensions={0} | all-to-all | bytes 12582912 | tf_op jit(solution)/shard_map/all_to_all | solution.py:44
  150.4 2.1 fusion.39
  152.5 0.6 slice-done.1
  153.1 3.5 %fusion.7 = f32[768,1024]{1,0:T(8,128)} fusion(bf16[768,1024]{1,0:T(8,128)(2,1)S(1)} %bitcast.53, bf16[1,4096,1024]{2,1,0:T(8,128)(2,1)S(1)} %bitcast.55), kind=kOutput, calls=%fused_computation.13 | convolution fusion | flops 1610612736 | bytes 6815744 | tf_op jit(solution)/shard_map/dot_general | solution.py:53
  156.6 3.5 %fusion.9 = f32[768,1024]{1,0:T(8,128)} fusion(bf16[768,1024]{1,0:T(8,128)(2,1)S(1)} %bitcast.52, bf16[1,4096,1024]{2,1,0:T(8,128)(2,1)S(1)} %bitcast.55), kind=kOutput, calls=%fused_computation.15 | convolution fusion | flops 1610612736 | bytes 6815744 | tf_op jit(solution)/shard_map/dot_general | solution.py:53
  160.1 3.5 %fusion.11 = f32[768,1024]{1,0:T(8,128)} fusion(bf16[768,1024]{1,0:T(8,128)(2,1)S(1)} %bitcast.51, bf16[1,4096,1024]{2,1,0:T(8,128)(2,1)S(1)} %bitcast.55), kind=kOutput, calls=%fused_computation.17 | convolution fusion | flops 1610612736 | bytes 6815744 | tf_op jit(solution)/shard_map/dot_general | solution.py:53
  163.6 9.5 %fusion.19 = bf16[768,1024]{1,0:T(8,128)(2,1)} fusion(bf16[1,1024,1024]{2,1,0:T(8,128)(2,1)S(1)} %copy-done, f32[768,1024]{1,0:T(8,128)} %fusion.7, f32[768,1024]{1,0:T(8,128)} %fusion.9, f32[768,1024]{1,0:T(8,128)} %fusion.11, bf16[768,1024]{1,0:T(8,128)(2,1)} %bitcast.50, bf16[1,4096,1024]{2,1,0:T(8,128)(2,1)} %param.10), kind=kOutput, calls=%fused_computation.25 | convolution fusion | flops 3225944064 | bytes 16777216 | tf_op jit(solution)/shard_map/dot_general | solution.py:59
  173.1 3.9 %reshape.29 = bf16[8,96,4,256]{3,2,1,0:T(4,128)(2,1)} reshape(bf16[768,1024]{1,0:T(8,128)(2,1)} %fusion.19) | data formatting | bytes 3145728 | tf_op jit(solution)/shard_map/reshape | solution.py:63
  177.0 2.8 %copy.7 = bf16[8,96,4,256]{3,1,2,0:T(8,128)(2,1)} copy(bf16[8,96,4,256]{3,2,1,0:T(4,128)(2,1)} %reshape.29) | data formatting | bytes 3145728 | tf_op jit(solution)/shard_map/reshape | solution.py:63
  179.8 5.9 %all-to-all-start.1 = ((bf16[32,96,256]{2,1,0:T(8,128)(2,1)}), bf16[32,96,256]{2,1,0:T(8,128)(2,1)}, u32[]{:S(2)}, u32[]{:S(2)}) async-start(bf16[32,96,256]{2,1,0:T(8,128)(2,1)} %bitcast.49), calls=%async_computation.1 | async-start | bytes 3145728 | tf_op jit(solution)/shard_map/all_to_all | solution.py:65
  185.8 2.0 fusion.40
  187.8 14.8 %all-gather = f32[3072,32]{0,1:T(8,128)S(1)} all-gather(f32[768,32]{0,1:T(8,128)S(1)} %fusion.40), channel_id=2, replica_groups=mesh['expert'=8,'gate'=4] {'gate'}, dimensions={0}, use_global_device_ids=true | all-gather | bytes 491520 | tf_op jit(solution)/shard_map/all_gather | solution.py:36
  202.6 0.2 reshape.32
  202.8 0.2 reduce_sum.54
  203.1 0.1 select_reduce_fusion.3
  203.2 18.2 %all-to-all-done.1 = bf16[32,96,256]{2,1,0:T(8,128)(2,1)} async-done(((bf16[32,96,256]{2,1,0:T(8,128)(2,1)}), bf16[32,96,256]{2,1,0:T(8,128)(2,1)}, u32[]{:S(2)}, u32[]{:S(2)}) %all-to-all-start.1) | async-done | bytes 1572896 | tf_op jit(solution)/shard_map/all_to_all | solution.py:65
  221.4 3.1 %fusion.23 = f32[768,256]{1,0:T(8,128)S(1)} fusion(bf16[3072,256]{1,0:T(8,128)(2,1)} %bitcast.15, s32[768]{0:T(1024)S(1)} %get-tuple-element.11, f32[768]{0:T(1024)S(1)} %get-tuple-element.19), kind=kOutput, calls=%fused_computation.27 | convolution fusion | flops 1210515456 | bytes 2365440 | tf_op jit(solution)/shard_map/dot_general | solution.py:75
  224.5 3.9 %fusion.26 = bf16[768,256]{1,0:T(8,128)(2,1)} fusion(f32[768,256]{1,0:T(8,128)S(1)} %fusion.23, bf16[3072,256]{1,0:T(8,128)(2,1)} %bitcast.15, s32[768]{0:T(1024)S(1)} %get-tuple-element.10, f32[768]{0:T(1024)S(1)} %get-tuple-element.18), kind=kOutput, calls=%fused_computation.30 | convolution fusion | flops 1210908672 | bytes 2758656 | tf_op jit(solution)/shard_map/dot_general | solution.py:75
  (18 shorter events, 0.1 us)
Async XLA Ops:
  0.0 163.6 %copy-start = (bf16[1,1024,1024]{2,1,0:T(8,128)(2,1)S(1)}, bf16[1,1024,1024]{2,1,0:T(8,128)(2,1)}, u32[]{:S(2)}) copy-start(bf16[1,1024,1024]{2,1,0:T(8,128)(2,1)} %param.11) | copy-start | bytes 6291460
  1.0 1.8 copy-start.1
  8.0 144.5 %slice-start = ((s8[8388608]{0:T(1024)(128)(4,1)}), s8[4194304]{0:T(1024)(128)(4,1)S(1)}, s32[]{:S(2)}) async-start(s8[8388608]{0:T(1024)(128)(4,1)} %bitcast.54), calls=%async_computation.2 | async-start | bytes 8388608
  150.4 2.8 %slice-start.1 = ((s8[8388608]{0:T(1024)(128)(4,1)}), s8[4194304]{0:T(1024)(128)(4,1)S(1)}, s32[]{:S(2)}) async-start(s8[8388608]{0:T(1024)(128)(4,1)} %bitcast.54), calls=%async_computation.3 | async-start | bytes 8388608
  179.8 6.0 %copy-start.2 = (bf16[1024,32]{0,1:T(8,128)(2,1)S(1)}, bf16[1024,32]{0,1:T(8,128)(2,1)}, u32[]{:S(2)}) copy-start(bf16[1024,32]{0,1:T(8,128)(2,1)} %param.7) | copy-start | bytes 196612
  179.8 41.6 %all-to-all-start.1 = ((bf16[32,96,256]{2,1,0:T(8,128)(2,1)}), bf16[32,96,256]{2,1,0:T(8,128)(2,1)}, u32[]{:S(2)}, u32[]{:S(2)}) async-start(bf16[32,96,256]{2,1,0:T(8,128)(2,1)} %bitcast.49), calls=%async_computation.1 | async-start | bytes 3145728 | tf_op jit(solution)/shard_map/all_to_all | solution.py:65
  185.8 17.3 %copy-start.3 = (s32[768,2]{0,1:T(2,128)S(1)}, s32[768,2]{0,1:T(2,128)}, u32[]{:S(2)}) copy-start(s32[768,2]{0,1:T(2,128)} %param.8) | copy-start | bytes 18436
  185.8 17.4 %copy-start.4 = (s32[768]{0:T(1024)S(1)}, s32[768]{0:T(1024)}, u32[]{:S(2)}) copy-start(s32[768]{0:T(1024)} %param.9) | copy-start | bytes 9220

commit v2 on v1

--- a/solution.py
+++ b/solution.py
@@ -1,7 +1,16 @@
+import functools
+
 import jax
 import jax.numpy as jnp
 from jax import lax
+from jax.experimental import pallas as pl
+from jax.experimental.pallas import tpu as pltpu
 from jax.sharding import PartitionSpec as P
+
+
+MESH = pl.DeviceIdType.MESH
+CHUNKS = 4
+SIDES = 2
 
 
 def routing(expert_ids, expert_count):
@@ -26,7 +35,415 @@
     return factor0, factor1
 
 
+def copied(source, target, sem):
+    return pltpu.make_async_copy(source, target, sem)
+
+
+def sent(source, target, send_sem, recv_sem, device):
+    return pltpu.make_async_remote_copy(
+        src_ref=source,
+        dst_ref=target,
+        send_sem=send_sem,
+        recv_sem=recv_sem,
+        device_id=device,
+        device_id_type=MESH,
+    )
+
+
+def table(values, index):
+    out = values[0]
+    for k in range(1, len(values)):
+        out = jnp.where(index == k, values[k], out)
+    return out
+
+
+def exchange_kernel(
+    planes,
+    gates,
+    capacity,
+    samples,
+    place,
+    partial,
+    up,
+    down,
+    ret,
+    logits,
+    blocks,
+    places,
+    onehot,
+    dbuf,
+    inc,
+    upv,
+    downv,
+    hidden,
+    obuf,
+    own_sem,
+    w_sem,
+    zs_up,
+    zs_down,
+    zs_relay,
+    zr,
+    ps,
+    pr,
+    rs,
+    rr,
+    ms,
+    mr,
+    gs,
+    gr,
+    l_sem,
+):
+    chunks = CHUNKS
+    local = SIDES * gates
+    e = lax.axis_index("expert")
+    g = lax.axis_index("gate")
+    z = e // SIDES
+    y = lax.rem(e, SIDES)
+    mine = y * gates + g
+    me = e * gates + g
+    total = planes * local
+    rows = blocks.shape[2]
+    width = blocks.shape[3]
+    slots = local * capacity
+
+    own = [
+        copied(samples.at[:, pl.ds(c * width, width)], blocks.at[z, c], own_sem.at[c])
+        for c in range(chunks)
+    ]
+    for copy in own:
+        copy.start()
+    weights = (copied(up.at[0], upv, w_sem.at[0]), copied(down.at[0], downv, w_sem.at[1]))
+    small = (
+        copied(place.at[pl.ds(z * local, local)], places.at[z], l_sem.at[0]),
+        copied(partial, logits.at[g], l_sem.at[1]),
+    )
+    for copy in small:
+        copy.start()
+
+    barrier = pltpu.get_barrier_semaphore()
+
+    def greet(d, carry):
+        t = lax.rem(me + d, total)
+        pl.semaphore_signal(
+            barrier, inc=1, device_id=(t // gates, lax.rem(t, gates)), device_id_type=MESH
+        )
+        return carry
+
+    lax.fori_loop(1, total, greet, 0)
+    pl.semaphore_wait(barrier, total - 1)
+
+    routes = []
+    for d in range(1, planes):
+        j = lax.rem(z + d, planes)
+        routes.append(
+            sent(
+                place.at[pl.ds(j * local, local)],
+                places.at[z],
+                ms.at[d - 1],
+                mr.at[z],
+                (j * SIDES + y, g),
+            )
+        )
+        routes[-1].start()
+    up_ok = z + 1 < planes
+    down_ok = z >= 1
+
+    def shift(j, c, sem, step):
+        return sent(
+            blocks.at[j, c], blocks.at[j, c], sem, zr.at[j, c], ((z + step) * SIDES + y, g)
+        )
+
+    for c in range(chunks):
+        own[c].wait()
+
+        @pl.when(up_ok)
+        def _():
+            shift(z, c, zs_up.at[c], 1).start()
+
+        @pl.when(down_ok)
+        def _():
+            shift(z, c, zs_down.at[c], -1).start()
+
+    for copy in weights:
+        copy.start()
+    gate_routes = []
+    for d in range(1, gates):
+        t = lax.rem(g + d, gates)
+        gate_routes.append(sent(partial, logits.at[g], gs.at[d - 1], gr.at[d - 1], (e, t)))
+        gate_routes[-1].start()
+    for copy in small:
+        copy.wait()
+
+    orders = [sorted(range(planes), key=lambda j: (abs(j - k), j)) for k in range(planes)]
+
+    def block_at(p):
+        return table([table(order, p) for order in orders], z)
+
+    def relay_up(j):
+        return (j < z) & up_ok
+
+    def relay_down(j):
+        return (j > z) & down_ok
+
+    items = planes * chunks
+
+    def dispatch(t):
+        j = block_at(t // chunks)
+        c = lax.rem(t, chunks)
+
+        @pl.when(j != z)
+        def _():
+            copied(blocks.at[j, c], blocks.at[j, c], zr.at[j, c]).wait()
+
+            @pl.when(relay_up(j))
+            def _():
+                shift(j, c, zs_relay.at[j, c], 1).start()
+
+            @pl.when(relay_down(j))
+            def _():
+                shift(j, c, zs_relay.at[j, c], -1).start()
+
+        @pl.when(c == 0)
+        def _():
+            @pl.when(j != z)
+            def _():
+                copied(places.at[j], places.at[j], mr.at[j]).wait()
+
+            ranks = lax.broadcasted_iota(jnp.int32, (capacity, rows), 0).astype(jnp.float32)
+            for i in range(local):
+                line = places[j, i : i + 1, :]
+                onehot[i * capacity : (i + 1) * capacity, :] = jnp.where(
+                    line == ranks, 1.0, 0.0
+                ).astype(jnp.bfloat16)
+
+        half = slots // 2
+        for h in range(2):
+            picked = jnp.dot(
+                onehot[h * half : (h + 1) * half, :],
+                blocks[j, c],
+                preferred_element_type=jnp.float32,
+            ).astype(jnp.bfloat16)
+            dbuf[j, c, h * half : (h + 1) * half, :] = picked
+
+        def give(d, carry):
+            i = lax.rem(mine + d, local)
+            sent(
+                dbuf.at[j, c, pl.ds(i * capacity, capacity)],
+                inc.at[j, c, g, pl.ds(y * capacity, capacity)],
+                ps,
+                pr.at[j, c],
+                (z * SIDES + i // gates, lax.rem(i, gates)),
+            ).start()
+            return carry
+
+        lax.fori_loop(1, local, give, 0)
+        copied(
+            dbuf.at[j, c, pl.ds(mine * capacity, capacity)],
+            inc.at[j, c, g, pl.ds(y * capacity, capacity)],
+            pr.at[j, c],
+        ).start()
+
+    def expert(t):
+        j = block_at(t // chunks)
+        c = lax.rem(t, chunks)
+        copied(inc.at[j, c], inc.at[j, c], pr.at[j, c]).wait()
+        share = width * chunks
+        tile = 256
+        for n in range(hidden.shape[1] // tile):
+            cols = slice(n * tile, (n + 1) * tile)
+            acc = jnp.zeros((SIDES * capacity, tile), jnp.float32)
+            for k in range(gates):
+                start = pl.multiple_of(k * share + c * width, width)
+                acc += jnp.dot(
+                    inc[j, c, k], upv[pl.ds(start, width), cols], preferred_element_type=jnp.float32
+                )
+
+            @pl.when(c == 0)
+            def _():
+                hidden[:, cols] = acc
+
+            @pl.when(c != 0)
+            def _():
+                hidden[:, cols] += acc
+
+        @pl.when(c == chunks - 1)
+        def _():
+            active = jnp.maximum(hidden[...], 0.0).astype(jnp.bfloat16)
+            out_width = downv.shape[1] // gates
+            for k in range(gates):
+                out = jnp.dot(
+                    active,
+                    downv[:, k * out_width : (k + 1) * out_width],
+                    preferred_element_type=jnp.float32,
+                ).astype(jnp.bfloat16)
+                obuf[j, k] = out
+
+            def hand(i, carry):
+                side, k = i // gates, lax.rem(i, gates)
+                block = obuf.at[j, k, pl.ds(side * capacity, capacity)]
+                away = (j != z) | (i != mine)
+
+                @pl.when(away)
+                def _():
+                    sent(block, ret.at[me], rs, rr.at[me], (j * SIDES + side, k)).start()
+
+                @pl.when(jnp.logical_not(away))
+                def _():
+                    copied(block, ret.at[me], rr.at[me]).start()
+
+                return carry
+
+            lax.fori_loop(0, local, hand, 0)
+
+    def step(t, carry):
+        @pl.when(t < items)
+        def _():
+            dispatch(t)
+
+        @pl.when(t == 1)
+        def _():
+            for copy in weights:
+                copy.wait()
+
+        @pl.when(t >= 1)
+        def _():
+            expert(t - 1)
+
+        return carry
+
+    lax.fori_loop(0, items + 1, step, 0)
+
+    for copy in routes + gate_routes:
+        copy.wait_send()
+    for copy in gate_routes:
+        copy.wait_recv()
+    for c in range(chunks):
+
+        @pl.when(up_ok)
+        def _():
+            shift(z, c, zs_up.at[c], 1).wait_send()
+
+        @pl.when(down_ok)
+        def _():
+            shift(z, c, zs_down.at[c], -1).wait_send()
+
+    def relayed(t, carry):
+        j, c = t // chunks, lax.rem(t, chunks)
+
+        @pl.when(relay_up(j) | relay_down(j))
+        def _():
+            copied(blocks.at[j, c], blocks.at[j, c], zs_relay.at[j, c]).wait()
+
+        return carry
+
+    lax.fori_loop(0, items, relayed, 0)
+    given = dbuf.at[:, :, pl.ds(0, slots - capacity)]
+    copied(given, given, ps).wait()
+    handed = ret.at[pl.ds(0, total - 1)]
+    copied(handed, handed, rs).wait()
+
+    def arrived(i, carry):
+        copied(ret.at[i], ret.at[i], rr.at[i]).wait()
+        return carry
+
+    lax.fori_loop(0, total, arrived, 0)
+
+
+def exchange(samples, place, partial, up, down, planes, gates, capacity):
+    rows, share = samples.shape
+    local = SIDES * gates
+    total = planes * local
+    width = share // CHUNKS
+    depth, inner = up.shape[1:]
+    outer = down.shape[2]
+    out_width = outer // gates
+    bf16, f32 = jnp.bfloat16, jnp.float32
+    dma = pltpu.SemaphoreType.DMA
+    vmem = pl.BlockSpec(memory_space=pltpu.VMEM)
+    hbm = pl.BlockSpec(memory_space=pl.ANY)
+    return pl.pallas_call(
+        functools.partial(exchange_kernel, planes, gates, capacity),
+        out_shape=(
+            jax.ShapeDtypeStruct((total, capacity, out_width), bf16),
+            jax.ShapeDtypeStruct((gates,) + partial.shape, f32),
+        ),
+        in_specs=[hbm, vmem, vmem, hbm, hbm],
+        out_specs=(vmem, vmem),
+        scratch_shapes=[
+            pltpu.VMEM((planes, CHUNKS, rows, width), bf16),
+            pltpu.VMEM((planes, local, rows), f32),
+            pltpu.VMEM((local * capacity, rows), bf16),
+            pltpu.VMEM((planes, CHUNKS, local * capacity, width), bf16),
+            pltpu.VMEM((planes, CHUNKS, gates, SIDES * capacity, width), bf16),
+            pltpu.VMEM((depth, inner), bf16),
+            pltpu.VMEM((inner, outer), bf16),
+            pltpu.VMEM((SIDES * capacity, inner), f32),
+            pltpu.VMEM((planes, gates, SIDES * capacity, out_width), bf16),
+            dma((CHUNKS,)),
+            dma((2,)),
+            dma((CHUNKS,)),
+            dma((CHUNKS,)),
+            dma((planes, CHUNKS)),
+            dma((planes, CHUNKS)),
+            dma,
+            dma((planes, CHUNKS)),
+            dma,
+            dma((total,)),
+            dma((planes,)),
+            dma((planes,)),
+            dma((gates,)),
+            dma((gates,)),
+            dma((2,)),
+        ],
+        compiler_params=pltpu.CompilerParams(
+            collective_id=0, has_side_effects=True, vmem_limit_bytes=56 << 20
+        ),
+    )(samples, place, partial, up, down)
+
+
+def combine(returned, expert_ids, first, second, before, factor0, factor1, capacity):
+    slots = jnp.arange(returned.shape[0], dtype=jnp.int32)[None, :]
+    mixed = 0.0
+    for k, (chosen, factor) in enumerate(((first, factor0), (second, factor1))):
+        rank = jnp.sum(jnp.where(chosen, before, 0), axis=1, keepdims=True)
+        position = expert_ids[:, k : k + 1] * capacity + rank
+        pick = (position == slots).astype(jnp.bfloat16)
+        mixed += factor * jnp.dot(pick, returned, preferred_element_type=jnp.float32)
+    return mixed.astype(jnp.bfloat16)
+
+
+def in_one_kernel(samples, gate_weight, expert_ids, pad_mask, up_weight, down_weight):
+    group_count = lax.axis_size("expert")
+    gate_count = lax.axis_size("gate")
+    expert_count = group_count * gate_count
+    capacity = 4 * samples.shape[0] // expert_count
+    partial = lax.dot_general(
+        gate_weight, samples, (((0,), (1,)), ((), ())), preferred_element_type=jnp.float32
+    )
+    first, second, member, before = routing(expert_ids, expert_count)
+    place = jnp.where(member, before, -1).T.astype(jnp.float32)
+    returned, logits = exchange(
+        samples, place, partial, up_weight, down_weight, group_count // SIDES, gate_count, capacity
+    )
+    returned = returned.reshape(expert_count * capacity, -1)
+    logits = jnp.sum(logits, axis=0).T
+    factor0, factor1 = factors(logits, first, second, pad_mask, expert_count)
+    return combine(returned, expert_ids, first, second, before, factor0, factor1, capacity)
+
+
+def fits(samples, up_weight, down_weight):
+    group_count = lax.axis_size("expert")
+    capacity = 4 * samples.shape[0] // (group_count * lax.axis_size("gate"))
+    planes = group_count // SIDES
+    held = 2 * (planes * samples.size * 3 + up_weight.size + down_weight.size)
+    return group_count % SIDES == 0 and capacity % 16 == 0 and held < 40 << 20
+
+
 def per_device(samples, gate_weight, expert_ids, pad_mask, up_weight, down_weight):
+    if fits(samples, up_weight, down_weight):
+        return in_one_kernel(
+            samples, gate_weight, expert_ids, pad_mask, up_weight, down_weight
+        )
     row_count, share = samples.shape
     group_count = lax.axis_size("expert")
     gate_count = lax.axis_size("gate")

time: 232 us -> 173 us (0.75); the launches traced: 228 us -> 172 us
  Pallas kernels: 0 us -> 161 us
  blocking collectives: 157 us -> 0 us
  matrix products: 34.6 us -> 9.33 us
  waiting for transfers between devices: 18.2 us -> 0 us
  local copies, waits for them, and re-layouts: 10.7 us -> 0.85 us
  starting transfers between devices: 5.94 us -> 0 us
    pallas_call x0 -> x1, Pallas kernels: none -> 161 us  [exchange(): pl.pallas_call(functools.partial(exchange_kernel, planes, gates, capacity...]
    all_to_all x1 -> x0, blocking collectives: 142 us -> none  [per_device(): lax.all_to_all(outgoing.reshape(expert_count, capacity, share), ('expert'...]
    dot_general x8 -> x3, matrix products: 34.3 us -> 8.34 us  [the longest x2 5.73 us: combine(): jnp.dot(pick, returned, preferred_element_type=jnp.float32)]
    all_to_all x1 -> x0, waiting for transfers between devices: 18.2 us -> none  [per_device(): lax.all_to_all(outbound, ('expert', 'gate'), split_axis=0, concat_axis=0,...]
    all_gather x1 -> x0, blocking collectives: 14.8 us -> none  [per_device(): logits = jnp.sum(lax.all_gather(partial, 'gate'), axis=0)]
    reshape x2 -> x0, local copies, waits for them, and re-layouts: 6.73 us -> none  [per_device(): outbound = expert_out.reshape(group_count, capacity, gate_count, out_share)]
    all_to_all x1 -> x0, starting transfers between devices: 5.94 us -> none  [per_device(): lax.all_to_all(outbound, ('expert', 'gate'), split_axis=0, concat_axis=0,...]
  transfers between devices with their start and end apart: 1 -> 0, of which waited for: 1 -> 0; matrix products, arithmetic and copies ran while one was open for 1% -> 0% of each run, Pallas kernels for 0% -> 0%
where the time goes in v2:
time: 173 us; the launch traced here: 172 us
  Pallas kernels  161 us (93%)
  matrix products  9.33 us (5%)
    pallas_call x1, Pallas kernels, exchange(): pl.pallas_call(functools.partial(exchange_kernel, planes, gates, capacity...  161 us
    dot_general x2, matrix products, combine(): jnp.dot(pick, returned, preferred_element_type=jnp.float32)  5.73 us

profile of v2, /device:TPU:31, one launch (start us, length us, event | category | flops | bytes accessed | tf_op | source)
XLA Modules:
  0.0 172.1 jit_solution(1339114470164446512)
XLA Ops:
  0.0 0.0 copy-start
  0.0 0.0 copy-start.1
  0.0 0.8 slice_reduce_fusion.1
  0.8 0.0 copy-done
  0.8 2.6 %fusion.19.partial = f32[32,768]{1,0:T(8,128)} fusion(bf16[1024,32]{0,1:T(8,128)(2,1)S(1)} %copy-done, bf16[768,1024]{1,0:T(8,128)(2,1)} %samples.1), kind=kOutput, calls=%fused_computation.38 | convolution fusion | flops 50331648 | bytes 1736704 | tf_op jit(solution)/shard_map/dot_general | solution.py:420
  3.5 1.0 fusion.12
  4.5 0.0 copy-done.1
  4.5 0.0 copy-start.2
  4.5 160.6 %shard_map.64 = (bf16[32,96,256]{2,1,0:T(8,128)(2,1)}, f32[4,32,768]{2,1,0:T(8,128)}) custom-call(bf16[768,1024]{1,0:T(8,128)(2,1)} %samples.1, f32[32,768]{1,0:T(8,128)} %get-tuple-element.19.place, f32[32,768]{1,0:T(8,128)} %fusion.19.partial, bf16[1,4096,1024]{2,1,0:T(8,128)(2,1)} %up.1, bf16[1,1024,1024]{2,1,0:T(8,128)(2,1)} %down.1), custom_call_target="tpu_custom_call" | custom-call | tf_op jit(solution)/shard_map/pallas_call | solution.py:364
  165.2 1.0 reduce_sum.54
  166.3 0.0 copy-done.2
  166.3 0.0 copy-start.3
  166.3 3.2 %fusion.5 = f32[768,256]{1,0:T(8,128)S(1)} fusion(bf16[3072,256]{1,0:T(8,128)(2,1)} %bitcast.16, s32[768]{0:T(1024)S(1)} %get-tuple-element.14, f32[768]{0:T(1024)S(1)} %get-tuple-element.18), kind=kOutput, calls=%fused_computation.8 | convolution fusion | flops 1210515456 | bytes 2365440 | tf_op jit(solution)/shard_map/dot_general | solution.py:411
  169.6 0.0 copy-done.3
  169.6 2.5 %fusion.8 = bf16[768,256]{1,0:T(8,128)(2,1)} fusion(f32[768,256]{1,0:T(8,128)S(1)} %fusion.5, bf16[3072,256]{1,0:T(8,128)(2,1)S(1)} %bitcast.17, s32[768]{0:T(1024)S(1)} %get-tuple-element.13, f32[768]{0:T(1024)S(1)} %get-tuple-element.17), kind=kOutput, calls=%fused_computation.11 | convolution fusion | flops 1210908672 | bytes 2758656 | tf_op jit(solution)/shard_map/dot_general | solution.py:411
  (6 shorter events, 0.2 us)
Async XLA Ops:
  0.0 0.8 copy-start
  0.0 4.5 %copy-start.1 = (s32[768,2]{0,1:T(2,128)S(1)}, s32[768,2]{0,1:T(2,128)}, u32[]{:S(2)}) copy-start(s32[768,2]{0,1:T(2,128)} %param.8) | copy-start | bytes 18436
  4.5 161.8 %copy-start.2 = (s32[768]{0:T(1024)S(1)}, s32[768]{0:T(1024)}, u32[]{:S(2)}) copy-start(s32[768]{0:T(1024)} %param.9) | copy-start | bytes 9220
  166.3 3.3 %copy-start.3 = (bf16[32,96,256]{2,1,0:T(8,128)(2,1)S(1)}, bf16[32,96,256]{2,1,0:T(8,128)(2,1)}, u32[]{:S(2)}) copy-start(bf16[32,96,256]{2,1,0:T(8,128)(2,1)} %get-tuple-element.8) | copy-start | bytes 4718596

commit v3 on v2

--- a/solution.py
+++ b/solution.py
@@ -63,7 +63,7 @@
     capacity,
     samples,
     place,
-    partial,
+    gate_weight,
     up,
     down,
     ret,
@@ -113,12 +113,8 @@
     for copy in own:
         copy.start()
     weights = (copied(up.at[0], upv, w_sem.at[0]), copied(down.at[0], downv, w_sem.at[1]))
-    small = (
-        copied(place.at[pl.ds(z * local, local)], places.at[z], l_sem.at[0]),
-        copied(partial, logits.at[g], l_sem.at[1]),
-    )
-    for copy in small:
-        copy.start()
+    kept = copied(place.at[pl.ds(z * local, local)], places.at[z], l_sem)
+    kept.start()
 
     barrier = pltpu.get_barrier_semaphore()
 
@@ -166,13 +162,20 @@
 
     for copy in weights:
         copy.start()
+    partial = 0.0
+    for c in range(chunks):
+        partial += lax.dot_general(
+            gate_weight[:, c * width : (c + 1) * width],
+            blocks[z, c],
+            (((1,), (1,)), ((), ())),
+            preferred_element_type=jnp.float32,
+        )
+    logits[g] = partial
+    kept.wait()
     gate_routes = []
     for d in range(1, gates):
         t = lax.rem(g + d, gates)
-        gate_routes.append(sent(partial, logits.at[g], gs.at[d - 1], gr.at[d - 1], (e, t)))
-        gate_routes[-1].start()
-    for copy in small:
-        copy.wait()
+        gate_routes.append(sent(logits.at[g], logits.at[g], gs.at[d - 1], gr.at[d - 1], (e, t)))
 
     orders = [sorted(range(planes), key=lambda j: (abs(j - k), j)) for k in range(planes)]
 
@@ -186,6 +189,27 @@
         return (j > z) & down_ok
 
     items = planes * chunks
+
+    def held_back(j):
+        return up_ok & down_ok & ((j == 0) | (j == planes - 1))
+
+    def give_back(j):
+        def hand(i, carry):
+            side, k = i // gates, lax.rem(i, gates)
+            block = obuf.at[j, k, pl.ds(side * capacity, capacity)]
+            away = (j != z) | (i != mine)
+
+            @pl.when(away)
+            def _():
+                sent(block, ret.at[me], rs, rr.at[me], (j * SIDES + side, k)).start()
+
+            @pl.when(jnp.logical_not(away))
+            def _():
+                copied(block, ret.at[me], rr.at[me]).start()
+
+            return carry
+
+        lax.fori_loop(0, local, hand, 0)
 
     def dispatch(t):
         j = block_at(t // chunks)
@@ -278,22 +302,9 @@
                 ).astype(jnp.bfloat16)
                 obuf[j, k] = out
 
-            def hand(i, carry):
-                side, k = i // gates, lax.rem(i, gates)
-                block = obuf.at[j, k, pl.ds(side * capacity, capacity)]
-                away = (j != z) | (i != mine)
-
-                @pl.when(away)
-                def _():
-                    sent(block, ret.at[me], rs, rr.at[me], (j * SIDES + side, k)).start()
-
-                @pl.when(jnp.logical_not(away))
-                def _():
-                    copied(block, ret.at[me], rr.at[me]).start()
-
-                return carry
-
-            lax.fori_loop(0, local, hand, 0)
+            @pl.when(jnp.logical_not(held_back(j)))
+            def _():
+                give_back(j)
 
     def step(t, carry):
         @pl.when(t < items)
@@ -302,6 +313,8 @@
 
         @pl.when(t == 1)
         def _():
+            for copy in gate_routes:
+                copy.start()
             for copy in weights:
                 copy.wait()
 
@@ -312,31 +325,37 @@
         return carry
 
     lax.fori_loop(0, items + 1, step, 0)
+
+    for c in range(chunks):
+
+        @pl.when(up_ok)
+        def _():
+            shift(z, c, zs_up.at[c], 1).wait_send()
+
+        @pl.when(down_ok)
+        def _():
+            shift(z, c, zs_down.at[c], -1).wait_send()
+
+    def relayed(t, carry):
+        j, c = t // chunks, lax.rem(t, chunks)
+
+        @pl.when(relay_up(j) | relay_down(j))
+        def _():
+            copied(blocks.at[j, c], blocks.at[j, c], zs_relay.at[j, c]).wait()
+
+        return carry
+
+    lax.fori_loop(0, items, relayed, 0)
+
+    @pl.when(up_ok & down_ok)
+    def _():
+        for j in (0, planes - 1):
+            give_back(j)
 
     for copy in routes + gate_routes:
         copy.wait_send()
     for copy in gate_routes:
         copy.wait_recv()
-    for c in range(chunks):
-
-        @pl.when(up_ok)
-        def _():
-            shift(z, c, zs_up.at[c], 1).wait_send()
-
-        @pl.when(down_ok)
-        def _():
-            shift(z, c, zs_down.at[c], -1).wait_send()
-
-    def relayed(t, carry):
-        j, c = t // chunks, lax.rem(t, chunks)
-
-        @pl.when(relay_up(j) | relay_down(j))
-        def _():
-            copied(blocks.at[j, c], blocks.at[j, c], zs_relay.at[j, c]).wait()
-
-        return carry
-
-    lax.fori_loop(0, items, relayed, 0)
     given = dbuf.at[:, :, pl.ds(0, slots - capacity)]
     copied(given, given, ps).wait()
     handed = ret.at[pl.ds(0, total - 1)]
@@ -349,7 +368,7 @@
     lax.fori_loop(0, total, arrived, 0)
 
 
-def exchange(samples, place, partial, up, down, planes, gates, capacity):
+def exchange(samples, place, gate_weight, up, down, planes, gates, capacity):
     rows, share = samples.shape
     local = SIDES * gates
     total = planes * local
@@ -365,7 +384,7 @@
         functools.partial(exchange_kernel, planes, gates, capacity),
         out_shape=(
             jax.ShapeDtypeStruct((total, capacity, out_width), bf16),
-            jax.ShapeDtypeStruct((gates,) + partial.shape, f32),
+            jax.ShapeDtypeStruct((gates, total, rows), f32),
         ),
         in_specs=[hbm, vmem, vmem, hbm, hbm],
         out_specs=(vmem, vmem),
@@ -393,12 +412,12 @@
             dma((planes,)),
             dma((gates,)),
             dma((gates,)),
-            dma((2,)),
+            dma,
         ],
         compiler_params=pltpu.CompilerParams(
             collective_id=0, has_side_effects=True, vmem_limit_bytes=56 << 20
         ),
-    )(samples, place, partial, up, down)
+    )(samples, place, gate_weight, up, down)
 
 
 def combine(returned, expert_ids, first, second, before, factor0, factor1, capacity):
@@ -417,13 +436,17 @@
     gate_count = lax.axis_size("gate")
     expert_count = group_count * gate_count
     capacity = 4 * samples.shape[0] // expert_count
-    partial = lax.dot_general(
-        gate_weight, samples, (((0,), (1,)), ((), ())), preferred_element_type=jnp.float32
-    )
     first, second, member, before = routing(expert_ids, expert_count)
     place = jnp.where(member, before, -1).T.astype(jnp.float32)
     returned, logits = exchange(
-        samples, place, partial, up_weight, down_weight, group_count // SIDES, gate_count, capacity
+        samples,
+        place,
+        gate_weight.T,
+        up_weight,
+        down_weight,
+        group_count // SIDES,
+        gate_count,
+        capacity,
     )
     returned = returned.reshape(expert_count * capacity, -1)
     logits = jnp.sum(logits, axis=0).T

time: 173 us -> 171 us (0.988)
  matrix products: 9.33 us -> 6.72 us
    dot_general x1 -> x0, matrix products: 2.62 us -> none  [in_one_kernel(): lax.dot_general(gate_weight, samples, (((0,), (1,)), ((), ())), preferred...]
where the time goes in v3:
time: 171 us
  Pallas kernels  161 us (94%)
  matrix products  6.72 us (4%)
  other arithmetic  1.97 us (1%)
    pallas_call x1, Pallas kernels, exchange(): pl.pallas_call(functools.partial(exchange_kernel, planes, gates, capacity...  161 us
    dot_general x2, matrix products, combine(): jnp.dot(pick, returned, preferred_element_type=jnp.float32)  5.72 us

profile of v3, /device:TPU:31, one launch (start us, length us, event | category | flops | bytes accessed | tf_op | source)
XLA Modules:
  0.0 170.6 jit_solution(11082127217740812970)
XLA Ops:
  0.0 0.8 slice_reduce_fusion.1
  0.8 1.0 fusion.12
  1.8 0.8 add_reduce_fusion.1
  2.6 0.0 copy-start
  2.6 161.0 %shard_map.64 = (bf16[32,96,256]{2,1,0:T(8,128)(2,1)}, f32[4,32,768]{2,1,0:T(8,128)}) custom-call(bf16[768,1024]{1,0:T(8,128)(2,1)} %samples.1, f32[32,768]{1,0:T(8,128)} %get-tuple-element.19.place, bf16[32,1024]{1,0:T(8,128)(2,1)} %bitcast.15, bf16[1,4096,1024]{2,1,0:T(8,128)(2,1)} %up.1, bf16[1,1024,1024]{2,1,0:T(8,128)(2,1)} %down.1), custom_call_target="tpu_custom_call" | custom-call | tf_op jit(solution)/shard_map/pallas_call | solution.py:383
  163.7 1.0 reduce_sum.54
  164.8 0.0 copy-done
  164.9 0.0 copy-start.1
  164.9 3.2 %fusion.5 = f32[768,256]{1,0:T(8,128)S(1)} fusion(bf16[3072,256]{1,0:T(8,128)(2,1)} %bitcast.16, s32[768]{0:T(1024)S(1)} %get-tuple-element.14, f32[768]{0:T(1024)S(1)} %get-tuple-element.18), kind=kOutput, calls=%fused_computation.8 | convolution fusion | flops 1210515456 | bytes 2365440 | tf_op jit(solution)/shard_map/dot_general | solution.py:430
  168.1 0.0 copy-done.1
  168.1 2.5 %fusion.8 = bf16[768,256]{1,0:T(8,128)(2,1)} fusion(f32[768,256]{1,0:T(8,128)S(1)} %fusion.5, bf16[3072,256]{1,0:T(8,128)(2,1)S(1)} %bitcast.17, s32[768]{0:T(1024)S(1)} %get-tuple-element.13, f32[768]{0:T(1024)S(1)} %get-tuple-element.17), kind=kOutput, calls=%fused_computation.11 | convolution fusion | flops 1210908672 | bytes 2758656 | tf_op jit(solution)/shard_map/dot_general | solution.py:430
  (5 shorter events, 0.1 us)
Async XLA Ops:
  2.6 162.2 %copy-start = (s32[768]{0:T(1024)S(1)}, s32[768]{0:T(1024)}, u32[]{:S(2)}) copy-start(s32[768]{0:T(1024)} %param.9) | copy-start | bytes 9220
  164.9 3.3 %copy-start.1 = (bf16[32,96,256]{2,1,0:T(8,128)(2,1)S(1)}, bf16[32,96,256]{2,1,0:T(8,128)(2,1)}, u32[]{:S(2)}) copy-start(bf16[32,96,256]{2,1,0:T(8,128)(2,1)} %get-tuple-element.8) | copy-start | bytes 4718596

commit v4 on v3

--- a/solution.py
+++ b/solution.py
@@ -211,9 +211,16 @@
 
         lax.fori_loop(0, local, hand, 0)
 
+    def item(t):
+        u = t - chunks
+        in_turn = up_ok & down_ok & (u >= 0) & (u < 2 * chunks)
+        p = jnp.where(in_turn, 1 + lax.rem(u + 2 * chunks, 2), t // chunks)
+        return p, jnp.where(in_turn, u // 2, lax.rem(t, chunks))
+
     def dispatch(t):
-        j = block_at(t // chunks)
-        c = lax.rem(t, chunks)
+        p, c = item(t)
+        j = block_at(p)
+        lane = lax.rem(p, 2)
 
         @pl.when(j != z)
         def _():
@@ -236,14 +243,14 @@
             ranks = lax.broadcasted_iota(jnp.int32, (capacity, rows), 0).astype(jnp.float32)
             for i in range(local):
                 line = places[j, i : i + 1, :]
-                onehot[i * capacity : (i + 1) * capacity, :] = jnp.where(
+                onehot[lane, i * capacity : (i + 1) * capacity, :] = jnp.where(
                     line == ranks, 1.0, 0.0
                 ).astype(jnp.bfloat16)
 
         half = slots // 2
         for h in range(2):
             picked = jnp.dot(
-                onehot[h * half : (h + 1) * half, :],
+                onehot[lane, h * half : (h + 1) * half, :],
                 blocks[j, c],
                 preferred_element_type=jnp.float32,
             ).astype(jnp.bfloat16)
@@ -268,12 +275,13 @@
         ).start()
 
     def expert(t):
-        j = block_at(t // chunks)
-        c = lax.rem(t, chunks)
+        p, c = item(t)
+        j = block_at(p)
+        lane = lax.rem(p, 2)
         copied(inc.at[j, c], inc.at[j, c], pr.at[j, c]).wait()
         share = width * chunks
         tile = 256
-        for n in range(hidden.shape[1] // tile):
+        for n in range(hidden.shape[2] // tile):
             cols = slice(n * tile, (n + 1) * tile)
             acc = jnp.zeros((SIDES * capacity, tile), jnp.float32)
             for k in range(gates):
@@ -284,15 +292,15 @@
 
             @pl.when(c == 0)
             def _():
-                hidden[:, cols] = acc
+                hidden[lane, :, cols] = acc
 
             @pl.when(c != 0)
             def _():
-                hidden[:, cols] += acc
+                hidden[lane, :, cols] += acc
 
         @pl.when(c == chunks - 1)
         def _():
-            active = jnp.maximum(hidden[...], 0.0).astype(jnp.bfloat16)
+            active = jnp.maximum(hidden[lane], 0.0).astype(jnp.bfloat16)
             out_width = downv.shape[1] // gates
             for k in range(gates):
                 out = jnp.dot(
@@ -391,12 +399,12 @@
         scratch_shapes=[
             pltpu.VMEM((planes, CHUNKS, rows, width), bf16),
             pltpu.VMEM((planes, local, rows), f32),
-            pltpu.VMEM((local * capacity, rows), bf16),
+            pltpu.VMEM((2, local * capacity, rows), bf16),
             pltpu.VMEM((planes, CHUNKS, local * capacity, width), bf16),
             pltpu.VMEM((planes, CHUNKS, gates, SIDES * capacity, width), bf16),
             pltpu.VMEM((depth, inner), bf16),
             pltpu.VMEM((inner, outer), bf16),
-            pltpu.VMEM((SIDES * capacity, inner), f32),
+            pltpu.VMEM((2, SIDES * capacity, inner), f32),
             pltpu.VMEM((planes, gates, SIDES * capacity, out_width), bf16),
             dma((CHUNKS,)),
             dma((2,)),

time: 171 us -> 153 us (0.89)
  Pallas kernels: 161 us -> 144 us
    pallas_call x1, Pallas kernels: 161 us -> 144 us  [exchange(): pl.pallas_call(functools.partial(exchange_kernel, planes, gates, capacity...]
where the time goes in v4:
time: 153 us
  Pallas kernels  144 us (94%)
  matrix products  6.72 us (4%)
  other arithmetic  1.97 us (1%)
    pallas_call x1, Pallas kernels, exchange(): pl.pallas_call(functools.partial(exchange_kernel, planes, gates, capacity...  144 us
    dot_general x2, matrix products, combine(): jnp.dot(pick, returned, preferred_element_type=jnp.float32)  5.73 us

profile of v4, /device:TPU:31, one launch (start us, length us, event | category | flops | bytes accessed | tf_op | source)
XLA Modules:
  0.0 153.1 jit_solution(13688522369328257385)
XLA Ops:
  0.0 0.8 slice_reduce_fusion.1
  0.8 1.0 fusion.12
  1.8 0.8 add_reduce_fusion.1
  2.6 0.0 copy-start
  2.6 143.6 %shard_map.64 = (bf16[32,96,256]{2,1,0:T(8,128)(2,1)}, f32[4,32,768]{2,1,0:T(8,128)}) custom-call(bf16[768,1024]{1,0:T(8,128)(2,1)} %samples.1, f32[32,768]{1,0:T(8,128)} %get-tuple-element.19.place, bf16[32,1024]{1,0:T(8,128)(2,1)} %bitcast.15, bf16[1,4096,1024]{2,1,0:T(8,128)(2,1)} %up.1, bf16[1,1024,1024]{2,1,0:T(8,128)(2,1)} %down.1), custom_call_target="tpu_custom_call" | custom-call | tf_op jit(solution)/shard_map/pallas_call | solution.py:391
  146.2 1.0 reduce_sum.54
  147.4 0.0 copy-done
  147.4 0.0 copy-start.1
  147.4 3.2 %fusion.5 = f32[768,256]{1,0:T(8,128)S(1)} fusion(bf16[3072,256]{1,0:T(8,128)(2,1)} %bitcast.16, s32[768]{0:T(1024)S(1)} %get-tuple-element.14, f32[768]{0:T(1024)S(1)} %get-tuple-element.18), kind=kOutput, calls=%fused_computation.8 | convolution fusion | flops 1210515456 | bytes 2365440 | tf_op jit(solution)/shard_map/dot_general | solution.py:438
  150.6 0.0 copy-done.1
  150.6 2.5 %fusion.8 = bf16[768,256]{1,0:T(8,128)(2,1)} fusion(f32[768,256]{1,0:T(8,128)S(1)} %fusion.5, bf16[3072,256]{1,0:T(8,128)(2,1)S(1)} %bitcast.17, s32[768]{0:T(1024)S(1)} %get-tuple-element.13, f32[768]{0:T(1024)S(1)} %get-tuple-element.17), kind=kOutput, calls=%fused_computation.11 | convolution fusion | flops 1210908672 | bytes 2758656 | tf_op jit(solution)/shard_map/dot_general | solution.py:438
  (5 shorter events, 0.1 us)
Async XLA Ops:
  2.6 144.7 %copy-start = (s32[768]{0:T(1024)S(1)}, s32[768]{0:T(1024)}, u32[]{:S(2)}) copy-start(s32[768]{0:T(1024)} %param.9) | copy-start | bytes 9220
  147.4 3.3 %copy-start.1 = (bf16[32,96,256]{2,1,0:T(8,128)(2,1)S(1)}, bf16[32,96,256]{2,1,0:T(8,128)(2,1)}, u32[]{:S(2)}) copy-start(bf16[32,96,256]{2,1,0:T(8,128)(2,1)} %get-tuple-element.8) | copy-start | bytes 4718596

commit v5 on v4

--- a/solution.py
+++ b/solution.py
@@ -62,12 +62,16 @@
     gates,
     capacity,
     samples,
-    place,
+    ids,
+    mask,
     gate_weight,
     up,
     down,
+    mixed,
     ret,
     logits,
+    place,
+    factor,
     blocks,
     places,
     onehot,
@@ -113,8 +117,6 @@
     for copy in own:
         copy.start()
     weights = (copied(up.at[0], upv, w_sem.at[0]), copied(down.at[0], downv, w_sem.at[1]))
-    kept = copied(place.at[pl.ds(z * local, local)], places.at[z], l_sem)
-    kept.start()
 
     barrier = pltpu.get_barrier_semaphore()
 
@@ -128,6 +130,47 @@
     lax.fori_loop(1, total, greet, 0)
     pl.semaphore_wait(barrier, total - 1)
 
+    up_ok = z + 1 < planes
+    down_ok = z >= 1
+
+    def shift(j, c, sem, step):
+        return sent(
+            blocks.at[j, c], blocks.at[j, c], sem, zr.at[j, c], ((z + step) * SIDES + y, g)
+        )
+
+    for c in range(chunks):
+        own[c].wait()
+
+        @pl.when(up_ok)
+        def _():
+            shift(z, c, zs_up.at[c], 1).start()
+
+        @pl.when(down_ok)
+        def _():
+            shift(z, c, zs_down.at[c], -1).start()
+
+    lanes = lax.broadcasted_iota(jnp.int32, (total, rows), 0)
+    member = (ids[0:1, :] == lanes) | (ids[1:2, :] == lanes)
+    earlier = lax.broadcasted_iota(jnp.int32, (rows, rows), 0) < lax.broadcasted_iota(
+        jnp.int32, (rows, rows), 1
+    )
+    before = jnp.dot(
+        jnp.where(member, 1.0, 0.0).astype(jnp.bfloat16),
+        jnp.where(earlier, 1.0, 0.0).astype(jnp.bfloat16),
+        preferred_element_type=jnp.float32,
+    )
+    place[...] = jnp.where(member, before, -1.0)
+    for copy in weights:
+        copy.start()
+    partial = 0.0
+    for c in range(chunks):
+        partial += lax.dot_general(
+            gate_weight[:, c * width : (c + 1) * width],
+            blocks[z, c],
+            (((1,), (1,)), ((), ())),
+            preferred_element_type=jnp.float32,
+        )
+    logits[g] = partial
     routes = []
     for d in range(1, planes):
         j = lax.rem(z + d, planes)
@@ -141,36 +184,8 @@
             )
         )
         routes[-1].start()
-    up_ok = z + 1 < planes
-    down_ok = z >= 1
-
-    def shift(j, c, sem, step):
-        return sent(
-            blocks.at[j, c], blocks.at[j, c], sem, zr.at[j, c], ((z + step) * SIDES + y, g)
-        )
-
-    for c in range(chunks):
-        own[c].wait()
-
-        @pl.when(up_ok)
-        def _():
-            shift(z, c, zs_up.at[c], 1).start()
-
-        @pl.when(down_ok)
-        def _():
-            shift(z, c, zs_down.at[c], -1).start()
-
-    for copy in weights:
-        copy.start()
-    partial = 0.0
-    for c in range(chunks):
-        partial += lax.dot_general(
-            gate_weight[:, c * width : (c + 1) * width],
-            blocks[z, c],
-            (((1,), (1,)), ((), ())),
-            preferred_element_type=jnp.float32,
-        )
-    logits[g] = partial
+    kept = copied(place.at[pl.ds(z * local, local)], places.at[z], l_sem)
+    kept.start()
     kept.wait()
     gate_routes = []
     for d in range(1, gates):
@@ -364,19 +379,57 @@
         copy.wait_send()
     for copy in gate_routes:
         copy.wait_recv()
+    logit = logits[0]
+    for k in range(1, gates):
+        logit += logits[k]
+    terms = jnp.exp(logit - jnp.max(logit, axis=0, keepdims=True))
+    scale = total * mask[...].astype(jnp.float32) / jnp.sum(terms, axis=0, keepdims=True)
+    factor[...] = jnp.where(place[...] >= 0.0, terms * scale, 0.0)
+
+    def collect(p, carry):
+        j = block_at(p)
+        start = pl.multiple_of(j * local, local)
+        places[j] = place[pl.ds(start, local), :]
+        weight = factor[pl.ds(start, local), :]
+        ranks = lax.broadcasted_iota(jnp.int32, (capacity, rows), 0).astype(jnp.float32)
+        for i in range(local):
+            chosen = places[j, i : i + 1, :] == ranks
+            exact = weight[i : i + 1, :]
+            high = exact.astype(jnp.bfloat16).astype(jnp.float32)
+            span = slice(i * capacity, (i + 1) * capacity)
+            onehot[0, span, :] = jnp.where(chosen, high, 0.0).astype(jnp.bfloat16)
+            onehot[1, span, :] = jnp.where(chosen, exact - high, 0.0).astype(jnp.bfloat16)
+
+        def arrived(i, inner):
+            copied(ret.at[start + i], ret.at[start + i], rr.at[start + i]).wait()
+            return inner
+
+        lax.fori_loop(0, local, arrived, 0)
+        back = ret[pl.ds(start, local)].reshape(slots, ret.shape[2])
+        part = 0.0
+        for k in range(2):
+            part += lax.dot_general(
+                onehot[k], back, (((0,), (0,)), ((), ())), preferred_element_type=jnp.float32
+            )
+
+        @pl.when(p == 0)
+        def _():
+            mixed[...] = part
+
+        @pl.when(p != 0)
+        def _():
+            mixed[...] += part
+
+        return carry
+
+    lax.fori_loop(0, planes, collect, 0)
     given = dbuf.at[:, :, pl.ds(0, slots - capacity)]
     copied(given, given, ps).wait()
     handed = ret.at[pl.ds(0, total - 1)]
     copied(handed, handed, rs).wait()
 
-    def arrived(i, carry):
-        copied(ret.at[i], ret.at[i], rr.at[i]).wait()
-        return carry
-
-    lax.fori_loop(0, total, arrived, 0)
-
-
-def exchange(samples, place, gate_weight, up, down, planes, gates, capacity):
+
+def exchange(samples, ids, mask, gate_weight, up, down, planes, gates, capacity):
     rows, share = samples.shape
     local = SIDES * gates
     total = planes * local
@@ -390,13 +443,14 @@
     hbm = pl.BlockSpec(memory_space=pl.ANY)
     return pl.pallas_call(
         functools.partial(exchange_kernel, planes, gates, capacity),
-        out_shape=(
-            jax.ShapeDtypeStruct((total, capacity, out_width), bf16),
-            jax.ShapeDtypeStruct((gates, total, rows), f32),
-        ),
-        in_specs=[hbm, vmem, vmem, hbm, hbm],
-        out_specs=(vmem, vmem),
+        out_shape=jax.ShapeDtypeStruct((rows, out_width), f32),
+        in_specs=[hbm, vmem, vmem, vmem, hbm, hbm],
+        out_specs=vmem,
         scratch_shapes=[
+            pltpu.VMEM((total, capacity, out_width), bf16),
+            pltpu.VMEM((gates, total, rows), f32),
+            pltpu.VMEM((total, rows), f32),
+            pltpu.VMEM((total, rows), f32),
             pltpu.VMEM((planes, CHUNKS, rows, width), bf16),
             pltpu.VMEM((planes, local, rows), f32),
             pltpu.VMEM((2, local * capacity, rows), bf16),
@@ -425,30 +479,17 @@
         compiler_params=pltpu.CompilerParams(
             collective_id=0, has_side_effects=True, vmem_limit_bytes=56 << 20
         ),
-    )(samples, place, gate_weight, up, down)
-
-
-def combine(returned, expert_ids, first, second, before, factor0, factor1, capacity):
-    slots = jnp.arange(returned.shape[0], dtype=jnp.int32)[None, :]
-    mixed = 0.0
-    for k, (chosen, factor) in enumerate(((first, factor0), (second, factor1))):
-        rank = jnp.sum(jnp.where(chosen, before, 0), axis=1, keepdims=True)
-        position = expert_ids[:, k : k + 1] * capacity + rank
-        pick = (position == slots).astype(jnp.bfloat16)
-        mixed += factor * jnp.dot(pick, returned, preferred_element_type=jnp.float32)
-    return mixed.astype(jnp.bfloat16)
+    )(samples, ids, mask, gate_weight, up, down)
 
 
 def in_one_kernel(samples, gate_weight, expert_ids, pad_mask, up_weight, down_weight):
     group_count = lax.axis_size("expert")
     gate_count = lax.axis_size("gate")
-    expert_count = group_count * gate_count
-    capacity = 4 * samples.shape[0] // expert_count
-    first, second, member, before = routing(expert_ids, expert_count)
-    place = jnp.where(member, before, -1).T.astype(jnp.float32)
-    returned, logits = exchange(
+    capacity = 4 * samples.shape[0] // (group_count * gate_count)
+    mixed = exchange(
         samples,
-        place,
+        expert_ids.T,
+        pad_mask[None, :],
         gate_weight.T,
         up_weight,
         down_weight,
@@ -456,10 +497,7 @@
         gate_count,
         capacity,
     )
-    returned = returned.reshape(expert_count * capacity, -1)
-    logits = jnp.sum(logits, axis=0).T
-    factor0, factor1 = factors(logits, first, second, pad_mask, expert_count)
-    return combine(returned, expert_ids, first, second, before, factor0, factor1, capacity)
+    return mixed.astype(jnp.bfloat16)
 
 
 def fits(samples, up_weight, down_weight):

time: 153 us -> 163 us (1.065)
  Pallas kernels: 144 us -> 160 us
  matrix products: 6.72 us -> 0 us
    pallas_call x1, Pallas kernels: 144 us -> 160 us  [exchange(): pl.pallas_call(functools.partial(exchange_kernel, planes, gates, capacity...]
    dot_general x3 -> x0, matrix products: 6.72 us -> none  [the longest x2 5.73 us: combine(): jnp.dot(pick, returned, preferred_element_type=jnp.float32)]
    convert_element_type x0 -> x1, other arithmetic: none -> 1.92 us  [in_one_kernel(): return mixed.astype(jnp.bfloat16)]
where the time goes in v5:
time: 163 us
  Pallas kernels  160 us (98%)
  other arithmetic  1.92 us (1%)
    pallas_call x1, Pallas kernels, exchange(): pl.pallas_call(functools.partial(exchange_kernel, planes, gates, capacity...  160 us

profile of v5, /device:TPU:31, one launch (start us, length us, event | category | flops | bytes accessed | tf_op | source)
XLA Modules:
  0.0 162.8 jit_solution(17139376511996446036)
XLA Ops:
  0.0 1.3 broadcast_in_dim.3.mask
  1.3 159.6 %shard_map.64 = f32[768,256]{1,0:T(8,128)} custom-call(bf16[768,1024]{1,0:T(8,128)(2,1)} %samples.1, s32[2,768]{1,0:T(2,128)} %bitcast.3, s32[1,768]{1,0:T(1,128)} %broadcast_in_dim.3.mask, bf16[32,1024]{1,0:T(8,128)(2,1)} %bitcast.2, bf16[1,4096,1024]{2,1,0:T(8,128)(2,1)} %up.1, bf16[1,1024,1024]{2,1,0:T(8,128)(2,1)} %down.1), custom_call_target="tpu_custom_call" | custom-call | tf_op jit(solution)/shard_map/pallas_call | solution.py:444
  160.8 1.9 %convert_element_type.3 = bf16[768,256]{1,0:T(8,128)(2,1)} convert(f32[768,256]{1,0:T(8,128)} %shard_map.64) | non-fusion elementwise | flops 196608 | bytes 1179648 | tf_op jit(solution)/shard_map/convert_element_type | solution.py:500

commit v6 on v5

--- a/solution.py
+++ b/solution.py
@@ -405,12 +405,10 @@
             return inner
 
         lax.fori_loop(0, local, arrived, 0)
-        back = ret[pl.ds(start, local)].reshape(slots, ret.shape[2])
+        back = ret[pl.ds(start, local)].reshape(slots, ret.shape[2]).T
         part = 0.0
         for k in range(2):
-            part += lax.dot_general(
-                onehot[k], back, (((0,), (0,)), ((), ())), preferred_element_type=jnp.float32
-            )
+            part += jnp.dot(back, onehot[k], preferred_element_type=jnp.float32)
 
         @pl.when(p == 0)
         def _():
@@ -443,7 +441,7 @@
     hbm = pl.BlockSpec(memory_space=pl.ANY)
     return pl.pallas_call(
         functools.partial(exchange_kernel, planes, gates, capacity),
-        out_shape=jax.ShapeDtypeStruct((rows, out_width), f32),
+        out_shape=jax.ShapeDtypeStruct((out_width, rows), f32),
         in_specs=[hbm, vmem, vmem, vmem, hbm, hbm],
         out_specs=vmem,
         scratch_shapes=[
@@ -497,7 +495,7 @@
         gate_count,
         capacity,
     )
-    return mixed.astype(jnp.bfloat16)
+    return mixed.T.astype(jnp.bfloat16)
 
 
 def fits(samples, up_weight, down_weight):

time: 163 us -> 163 us (level)
  no operation moved by 1% of the time
where the time goes in v6:
time: 163 us
  Pallas kernels  160 us (98%)
  local copies, waits for them, and re-layouts  2.19 us (1%)
    pallas_call x1, Pallas kernels, exchange(): pl.pallas_call(functools.partial(exchange_kernel, planes, gates, capacity...  160 us

profile of v6, /device:TPU:31, one launch (start us, length us, event | category | flops | bytes accessed | tf_op | source)
XLA Modules:
  0.0 162.9 jit_solution(7952171778856375566)
XLA Ops:
  0.0 1.3 broadcast_in_dim.3.mask
  1.3 159.5 %shard_map.64 = f32[256,768]{1,0:T(8,128)} custom-call(bf16[768,1024]{1,0:T(8,128)(2,1)} %samples.1, s32[2,768]{1,0:T(2,128)} %bitcast.5, s32[1,768]{1,0:T(1,128)} %broadcast_in_dim.3.mask, bf16[32,1024]{1,0:T(8,128)(2,1)} %bitcast.4, bf16[1,4096,1024]{2,1,0:T(8,128)(2,1)} %up.1, bf16[1,1024,1024]{2,1,0:T(8,128)(2,1)} %down.1), custom_call_target="tpu_custom_call" | custom-call | tf_op jit(solution)/shard_map/pallas_call | solution.py:442
  160.8 1.2 convert_bitcast_fusion
  162.0 0.9 copy.7
